TPU v7x, 128 devices: a whole 4x4x4 slice. The times are simulated.
128 devices in a mesh: row: 16 (over x, z_lo, core), col: 8 (over y, z_hi).
Axes of the slice: x: 4, y: 4, z: 4 (z_hi: 2, z_lo: 2; z = z_hi * 2 + z_lo), core: 2. Of those that a mesh axis runs over, the one named last changes fastest.
Arguments:
- source: float32 [512, 512, 512], P('row', 'col'), may hold values from -8 to 8
- basis_x: float32 [512, 512], replicated, may hold values from -0.25 to 0.25
- basis_y: float32 [512, 512], replicated, may hold values from -0.25 to 0.25
- basis_z: float32 [512, 512], replicated, may hold values from -0.25 to 0.25
- eigen_x: float32 [512], replicated, may hold values from 0.1 to 10
- eigen_y: float32 [512], replicated, may hold values from 0.1 to 10
- eigen_z: float32 [512], replicated, may hold values from 0.1 to 10
Outputs:
- solution: float32 [512, 512, 512], P('row', 'col')
All inputs are finite; a program needn't handle non-finite values.
Results may differ from a plain program's by a relative error of at most 0.00007.
Values sent between devices are 32-bit elements; how exact they have to be, the bound alone decides.
No kernel may reach another device: no remote copies, remote signals or barrier semaphores. Data moves between devices by JAX's collectives and lax.ppermute only.
A program may use at most 128 MiB of HBM per device.

v0:
```python
import jax
import jax.numpy as jnp
from jax import lax
from jax.sharding import PartitionSpec as P

HIGH = lax.Precision.HIGHEST


def divide(field, first, second, third):
    denom = first[:, None, None] + second[None, :, None] + third[None, None, :]
    return field / denom


def piece_of(values, index, count):
    return lax.dynamic_slice_in_dim(values, index * count, count, 0)


def local(source, basis_x, basis_y, basis_z, eigen_x, eigen_y, eigen_z):
    row_index = lax.axis_index("row")
    col_index = lax.axis_index("col")
    rows_n = lax.axis_size("row")
    cols_n = lax.axis_size("col")
    nx_full = basis_x.shape[0]
    ny_full = basis_y.shape[0]
    field = jnp.einsum("ck,abc->abk", basis_z, source, precision=HIGH)
    field = field[None]
    field = lax.all_to_all(field, ("row", "col"), split_axis=3, concat_axis=0, tiled=True)
    planes = field.shape[3]
    field = field.reshape(rows_n, cols_n, field.shape[1], field.shape[2], planes)
    blocks_x = basis_x.reshape(rows_n, nx_full // rows_n, nx_full)
    blocks_y = basis_y.reshape(cols_n, ny_full // cols_n, ny_full)
    field = jnp.einsum("rai,rcabk->icbk", blocks_x, field, precision=HIGH)
    field = jnp.einsum("cbj,icbk->ijk", blocks_y, field, precision=HIGH)
    part_z = piece_of(eigen_z, row_index * cols_n + col_index, planes)
    field = divide(field, eigen_x, eigen_y, part_z)
    field = jnp.einsum("cbj,ijk->icbk", blocks_y, field, precision=HIGH)
    field = jnp.einsum("rai,icbk->rcabk", blocks_x, field, precision=HIGH)
    field = field.reshape(rows_n * cols_n, field.shape[2], field.shape[3], planes)
    field = lax.all_to_all(field, ("row", "col"), split_axis=0, concat_axis=3, tiled=True)
    field = jnp.einsum("ck,abk->abc", basis_z, field[0], precision=HIGH)
    return field


def solution(mesh):
    placed = (P("row", "col", None), P(), P(), P(), P(), P(), P())
    return jax.shard_map(
        local, mesh=mesh, in_specs=placed, out_specs=P("row", "col", None), check_vma=False
    )
```

profile of v0, /device:TPU:1, one launch (start us, length us, event | category | flops | bytes accessed | tf_op | source)
XLA Modules:
  0.0 286.4 jit_solution(4744096187982554309)
XLA Ops:
  0.0 0.0 copy-start
  0.0 10.2 %convolution_bitcast_fusion = f32[1,32,64,512]{3,2,1,0:T(8,128)} fusion(f32[32,64,512]{2,1,0:T(8,128)} %param.7, f32[512,512]{1,0:T(8,128)} %param.10), kind=kOutput, calls=%fused_computation.13 | convolution fusion | flops 6442450944 | bytes 9437184 | tf_op jit(solution)/shard_map/ck,abc->abk/dot_general | solution.py:25
  10.2 9.1 %copy.11 = f32[1,32,64,512]{2,1,0,3:T(8,128)} copy(f32[1,32,64,512]{3,2,1,0:T(8,128)} %convolution_bitcast_fusion) | data formatting | bytes 8388608 | tf_op jit(solution)/shard_map/broadcast_in_dim | solution.py:26
  19.3 9.4 %reshape.58 = f32[128,1,8192]{2,1,0:T(1,128)} reshape(f32[512,1,32,64]{3,2,1,0:T(8,128)} %bitcast.72) | data formatting | bytes 8388608
  28.7 0.0 copy-start.4
  28.7 0.0 copy-start.5
  28.7 12.3 %all-to-all-start = ((f32[128,1,8192]{2,1,0:T(1,128)}), f32[128,1,8192]{2,1,0:T(1,128)}, u32[]{:S(2)}, u32[]{:S(2)}) async-start(f32[128,1,8192]{2,1,0:T(1,128)} %reshape.58), calls=%async_computation | async-start | bytes 8388608 | tf_op jit(solution)/shard_map/all_to_all | solution.py:27
  41.0 0.8 dynamic_slice.3
  41.8 0.0 copy-done.4
  41.8 0.0 copy-done.5
  41.8 0.1 broadcast_add_fusion
  41.9 50.6 %all-to-all-done = f32[128,1,8192]{2,1,0:T(1,128)} async-done(((f32[128,1,8192]{2,1,0:T(1,128)}), f32[128,1,8192]{2,1,0:T(1,128)}, u32[]{:S(2)}, u32[]{:S(2)}) %all-to-all-start) | async-done | bytes 4194336 | tf_op jit(solution)/shard_map/all_to_all | solution.py:27
  92.5 0.5 broadcast.24
  93.0 13.8 %reduce = f32[128,8192]{1,0:T(8,128)} reduce(f32[128,1,8192]{2,1,0:T(1,128)} %all-to-all-done, f32[]{:T(128)} %broadcast.24), dimensions={1}, to_apply=%all_to_all.22.reduce_sub_computation | reduce | bytes 8388612 | tf_op jit(solution)/shard_map/all_to_all | solution.py:27
  106.9 0.0 copy-start.2
  106.9 8.0 %reshape.59 = f32[512,1,32,64]{3,2,1,0:T(8,128)} reshape(f32[128,8192]{1,0:T(8,128)} %reduce) | data formatting | bytes 8388608
  114.8 0.0 copy-done.2
  114.8 17.0 %fusion = f32[8,64,4,512,1]{3,1,0,2,4:T(8,128)S(1)} fusion(f32[16,32,512,1,1]{2,1,3,4,0:T(8,128)S(1)} %bitcast.75, f32[16,8,32,64,4]{3,2,4,1,0:T(8,128)} %bitcast.71), kind=kOutput, calls=%fused_computation | convolution fusion | flops 6442450944 | bytes 9437184 | tf_op jit(solution)/shard_map/rai,rcabk->icbk/dot_general | solution.py:32
  131.9 0.0 copy-done
  131.9 6.7 %fusion.9 = f32[512,4,512,1]{2,0,3,1:T(8,128)S(1)} fusion(f32[8,64,512,1]{2,1,0,3:T(8,128)S(1)} %bitcast.70, f32[8,64,4,512,1]{3,1,0,2,4:T(8,128)S(1)} %fusion), kind=kOutput, calls=%fused_computation.9 | convolution fusion | flops 6442450944 | bytes 9437184 | tf_op jit(solution)/shard_map/cbj,icbk->ijk/dot_general | solution.py:33
  138.6 7.3 %fusion.5 = f32[512,4,8,64]{0,3,1,2:T(8,128)S(1)} fusion(f32[8,64,512,1]{2,1,3,0:T(8,128)S(1)} %bitcast.69, f32[512,4,512,1]{2,0,3,1:T(8,128)S(1)} %fusion.9, f32[4]{0:T(128)S(1)} %dynamic_slice.3, f32[512,512]{1,0:T(8,128)S(1)} %broadcast_add_fusion), kind=kOutput, calls=%fused_computation.6 | convolution fusion | flops 6444548096 | bytes 10485776 | tf_op jit(solution)/shard_map/cbj,ijk->icbk/dot_general | solution.py:36
  145.9 13.8 %fusion.12 = f32[16,8,32,64,4]{3,2,0,4,1:T(8,128)S(1)} fusion(f32[16,32,512,1,1]{2,1,0,4,3:T(8,128)S(1)} %bitcast.76, f32[512,4,8,64]{0,3,1,2:T(8,128)S(1)} %fusion.5), kind=kOutput, calls=%fused_computation.12 | convolution fusion | flops 6442450944 | bytes 9437184 | tf_op jit(solution)/shard_map/rai,icbk->rcabk/dot_general | solution.py:37
  159.7 4.3 %copy.13 = f32[16,8,32,64,4]{3,2,4,1,0:T(8,128)} copy(f32[16,8,32,64,4]{3,2,0,4,1:T(8,128)S(1)} %fusion.12) | data formatting | bytes 8388608 | tf_op jit(solution)/shard_map/rai,icbk->rcabk/transpose | solution.py:37
  164.0 9.4 %reshape.60 = f32[128,1,8192]{2,1,0:T(1,128)} reshape(f32[128,4,32,64]{3,2,1,0:T(8,128)} %bitcast.73) | data formatting | bytes 8388608
  173.4 58.1 %all_to_all.30 = f32[128,1,8192]{2,1,0:T(1,128)} all-to-all(f32[128,1,8192]{2,1,0:T(1,128)} %reshape.60), channel_id=1, replica_groups=mesh['row'=16,'col'=8] {'row','col'}, dimensions={0} | all-to-all | bytes 8388608 | tf_op jit(solution)/shard_map/all_to_all | solution.py:39
  231.5 13.8 %reduce.1 = f32[128,8192]{1,0:T(8,128)} reduce(f32[128,1,8192]{2,1,0:T(1,128)} %all_to_all.30, f32[]{:T(128)} %broadcast.24), dimensions={1}, to_apply=%all_to_all.25.reduce_sub_computation | reduce | bytes 8388612 | tf_op jit(solution)/shard_map/all_to_all | solution.py:39
  245.3 0.0 copy-start.3
  245.3 8.0 %reshape.61 = f32[128,4,32,64]{3,2,1,0:T(8,128)} reshape(f32[128,8192]{1,0:T(8,128)} %reduce.1) | data formatting | bytes 8388608
  253.3 0.0 copy-start.1
  253.3 0.0 copy-done.3
  253.3 32.7 %fusion.2 = f32[32,64,512]{2,1,0:T(8,128)} fusion(f32[32,64,512]{1,0,2:T(8,128)} %bitcast.74, f32[512,512]{1,0:T(8,128)S(1)} %copy-done.3), kind=kOutput, calls=%fused_computation.2 | convolution fusion | flops 6442450944 | bytes 9437184 | tf_op jit(solution)/shard_map/ck,abk->abc/dot_general | solution.py:40
  286.0 0.0 copy-done.1
Async XLA Ops:
  0.0 131.9 %copy-start = (f32[512,512]{1,0:T(8,128)S(1)}, f32[512,512]{1,0:T(8,128)}, u32[]{:S(2)}) copy-start(f32[512,512]{1,0:T(8,128)} %param.9) | copy-start | bytes 3145732
  28.7 13.1 %copy-start.4 = (f32[512]{0:T(512)S(1)}, f32[512]{0:T(512)}, u32[]{:S(2)}) copy-start(f32[512]{0:T(512)} %param.12) | copy-start | bytes 6148
  28.7 13.1 %copy-start.5 = (f32[512]{0:T(512)S(1)}, f32[512]{0:T(512)}, u32[]{:S(2)}) copy-start(f32[512]{0:T(512)} %param.11) | copy-start | bytes 6148
  28.7 63.8 %all-to-all-start = ((f32[128,1,8192]{2,1,0:T(1,128)}), f32[128,1,8192]{2,1,0:T(1,128)}, u32[]{:S(2)}, u32[]{:S(2)}) async-start(f32[128,1,8192]{2,1,0:T(1,128)} %reshape.58), calls=%async_computation | async-start | bytes 8388608 | tf_op jit(solution)/shard_map/all_to_all | solution.py:27
  106.9 8.0 %copy-start.2 = (f32[512,512]{1,0:T(8,128)S(1)}, f32[512,512]{1,0:T(8,128)}, u32[]{:S(2)}) copy-start(f32[512,512]{1,0:T(8,128)} %param.8) | copy-start | bytes 3145732
  245.3 8.0 %copy-start.3 = (f32[512,512]{1,0:T(8,128)S(1)}, f32[512,512]{1,0:T(8,128)}, u32[]{:S(2)}) copy-start(f32[512,512]{1,0:T(8,128)} %param.10) | copy-start | bytes 3145732
  253.3 32.7 %copy-start.1 = (f32[512,512]{1,0:T(8,128)S(1)}, f32[512,512]{1,0:T(8,128)}, u32[]{:S(2)}) copy-start(f32[512,512]{1,0:T(8,128)} %param.9) | copy-start | bytes 3145732
where the time goes:
time: 292 us; the launch traced here: 286 us
  matrix products  87.7 us (30%)
  blocking collectives  58.1 us (20%)
  waiting for transfers between devices  50.6 us (17%)
  local copies, waits for them, and re-layouts  49.4 us (17%)
  other arithmetic  27.8 us (10%)
  starting transfers between devices  12.3 us (4%)
    all_to_all x1, blocking collectives, local(): lax.all_to_all(field, ('row', 'col'), split_axis=0, concat_axis=3, tiled=...  58.1 us
    all_to_all x1, waiting for transfers between devices, local(): lax.all_to_all(field, ('row', 'col'), split_axis=3, concat_axis=0, tiled=...  50.6 us
    unnamed x16, local copies, waits for them, and re-layouts  34.7 us
    dot_general x1, matrix products, local(): field = jnp.einsum('ck,abk->abc', basis_z, field[0], precision=HIGH)  32.7 us
    dot_general x1, matrix products, local(): field = jnp.einsum('rai,rcabk->icbk', blocks_x, field, precision=HIGH)  17 us
    all_to_all x1, other arithmetic, local(): lax.all_to_all(field, ('row', 'col'), split_axis=0, concat_axis=3, tiled=...  13.8 us
    all_to_all x1, other arithmetic, local(): lax.all_to_all(field, ('row', 'col'), split_axis=3, concat_axis=0, tiled=...  13.8 us
    dot_general x1, matrix products, local(): field = jnp.einsum('rai,icbk->rcabk', blocks_x, field, precision=HIGH)  13.8 us
  transfers between devices with their start and end apart: 1, of which 1 were waited for; matrix products, arithmetic and copies ran while one was open for 0% of the time, Pallas kernels for 0%

commit v1 on v0

v1 whole, which is shorter than its diff:
```python
import functools

import jax
import jax.numpy as jnp
from jax import lax
from jax.experimental import pallas as pl
from jax.experimental.pallas import tpu as pltpu
from jax.sharding import PartitionSpec as P

F32 = jnp.float32
BF16 = jnp.bfloat16
AXES = ("row", "col")
NT = (((1,), (1,)), ((), ()))
NN = (((1,), (0,)), ((), ()))


def halves(value):
    high = value.astype(BF16)
    low = (value - high.astype(F32)).astype(BF16)
    return high, low


def product(left, right, dims=NN):
    return lax.dot_general(left, right, dims, preferred_element_type=F32)


def product3(left, right, dims=NN):
    left_high, left_low = left
    right_high, right_low = right
    return (
        product(left_high, right_high, dims)
        + product(left_high, right_low, dims)
        + product(left_low, right_high, dims)
    )


def forward_z(source_ref, basis_ref, out_ref, high_ref, low_ref):
    @pl.when(pl.program_id(0) == 0)
    def _():
        high_ref[...], low_ref[...] = halves(basis_ref[...].T)

    n_z = basis_ref.shape[0]
    flat = out_ref.reshape(n_z * 8, 128)
    for pair in range(4):
        part = halves(source_ref[pl.ds(pair * 256, 256), :])
        result = product3((high_ref[...], low_ref[...]), part, NT)
        flat[pl.ds(2 * pair, n_z, stride=8), :] = result[:, :128]
        flat[pl.ds(2 * pair + 1, n_z, stride=8), :] = result[:, 128:]


def backward_z(field_ref, basis_ref, out_ref, high_ref, low_ref):
    @pl.when(pl.program_id(0) == 0)
    def _():
        high_ref[...], low_ref[...] = halves(basis_ref[...].T)

    n_z = basis_ref.shape[0]
    flat = field_ref.reshape(n_z * 8, 128)
    for pair in range(4):
        lines = jnp.concatenate(
            [flat[pl.ds(2 * pair + side, n_z, stride=8), :].T for side in range(2)], axis=0
        )
        out_ref[pl.ds(pair * 256, 256), :] = product3(
            halves(lines), (high_ref[...], low_ref[...])
        )


def prepare(
    basis_x, basis_y, eigen_x,
    xt_high, xt_low, x_high, x_low, y_high, y_low, yt_high, yt_low, column, strips,
):
    half = basis_x.shape[0] // 2
    for strip in range(strips.shape[0]):
        strips[strip] = basis_x[:, pl.ds(strip * 128, 128)]
    ordered = jnp.concatenate(
        [
            jnp.concatenate(
                [strips[strip, pl.ds(side, half, stride=2), :] for strip in range(strips.shape[0])],
                axis=1,
            )
            for side in range(2)
        ],
        axis=0,
    )
    x_high[...], x_low[...] = halves(ordered)
    xt_high[...], xt_low[...] = halves(ordered.T)
    y_high[...], y_low[...] = halves(basis_y[...])
    yt_high[...], yt_low[...] = halves(basis_y[...].T)
    column[...] = jnp.broadcast_to(eigen_x[...], (128, eigen_x.shape[1])).T


def planes(
    field_ref, xt_high, xt_low, x_high, x_low, y_high, y_low, yt_high, yt_low,
    column, eigen_y, part_z, out_ref, plane_high, plane_low,
):
    rows_n, cols_n = field_ref.shape[0], field_ref.shape[1]
    half = rows_n * 16
    first = lax.broadcasted_iota(jnp.int32, (half, 128), 1) < 64
    for pair in range(cols_n // 2):
        left = field_ref[:, 2 * pair].reshape(half, 128)
        right = field_ref[:, 2 * pair + 1].reshape(half, 128)
        even = jnp.where(first, left, pltpu.roll(right, 64, 1))
        odd = jnp.where(first, pltpu.roll(left, 64, 1), right)
        at = pl.ds(pair * 128, 128)
        plane_high[pl.ds(0, half), at], plane_low[pl.ds(0, half), at] = halves(even)
        plane_high[pl.ds(half, half), at], plane_low[pl.ds(half, half), at] = halves(odd)
    field = product3((xt_high[...], xt_low[...]), (plane_high[...], plane_low[...]))
    field = product3(halves(field), (y_high[...], y_low[...]))
    denom = column[:, :1] + (eigen_y[...] + part_z[pl.program_id(0)])
    field = field / denom
    field = product3(halves(field), (yt_high[...], yt_low[...]))
    field = product3((x_high[...], x_low[...]), halves(field))
    for pair in range(cols_n // 2):
        even = field[:half, pair * 128 : pair * 128 + 128]
        odd = field[half:, pair * 128 : pair * 128 + 128]
        left = jnp.where(first, even, pltpu.roll(odd, 64, 1))
        right = jnp.where(first, pltpu.roll(even, 64, 1), odd)
        out_ref[:, 2 * pair] = left.reshape(rows_n, 2, 1, 8, 128)
        out_ref[:, 2 * pair + 1] = right.reshape(rows_n, 2, 1, 8, 128)


def whole(shape):
    return pl.BlockSpec(shape, lambda step: (0,) * len(shape))


def local(source, basis_x, basis_y, basis_z, eigen_x, eigen_y, eigen_z):
    rows_n, cols_n = lax.axis_size("row"), lax.axis_size("col")
    devices = rows_n * cols_n
    n = basis_z.shape[0]
    square = (n, n)
    lines = source.shape[0] * source.shape[1]
    params = pltpu.CompilerParams(dimension_semantics=("arbitrary",))

    sent = pl.pallas_call(
        forward_z,
        out_shape=jax.ShapeDtypeStruct((devices, 64, 128), F32),
        grid=(2,),
        in_specs=[pl.BlockSpec((lines // 2, n), lambda step: (step, 0)), whole(square)],
        out_specs=pl.BlockSpec((devices, 32, 128), lambda step: (0, step, 0)),
        scratch_shapes=[pltpu.VMEM(square, BF16)] * 2,
        compiler_params=params,
        name="forward_z",
    )(source.reshape(lines, n), basis_z)
    field = lax.all_to_all(sent, AXES, split_axis=0, concat_axis=0, tiled=True)

    tables = pl.pallas_call(
        prepare,
        out_shape=[jax.ShapeDtypeStruct(square, BF16)] * 8 + [jax.ShapeDtypeStruct((n, 128), F32)],
        scratch_shapes=[pltpu.VMEM((n // 128, n, 128), F32)],
        name="prepare",
    )(basis_x, basis_y, eigen_x.reshape(1, n))
    device = lax.axis_index("row") * cols_n + lax.axis_index("col")
    part_z = lax.dynamic_slice_in_dim(eigen_z, device * 4, 4, 0)
    block = pl.BlockSpec((rows_n, cols_n, 2, 1, 8, 128), lambda step: (0, 0, 0, step, 0, 0))
    shape = (rows_n, cols_n, 2, 4, 8, 128)
    field = pl.pallas_call(
        planes,
        out_shape=jax.ShapeDtypeStruct(shape, F32),
        grid=(4,),
        in_specs=[block]
        + [whole(square)] * 8
        + [whole((n, 128)), whole((1, n)), pl.BlockSpec(memory_space=pltpu.SMEM)],
        out_specs=block,
        scratch_shapes=[pltpu.VMEM(square, BF16)] * 2,
        compiler_params=params,
        name="planes",
    )(field.reshape(shape), *tables, eigen_y.reshape(1, n), part_z)

    field = field.reshape(devices, 64, 128)
    field = lax.all_to_all(field, AXES, split_axis=0, concat_axis=0, tiled=True)
    out = pl.pallas_call(
        backward_z,
        out_shape=jax.ShapeDtypeStruct((lines, n), F32),
        grid=(2,),
        in_specs=[pl.BlockSpec((devices, 32, 128), lambda step: (0, step, 0)), whole(square)],
        out_specs=pl.BlockSpec((lines // 2, n), lambda step: (step, 0)),
        scratch_shapes=[pltpu.VMEM(square, BF16)] * 2,
        compiler_params=params,
        name="backward_z",
    )(field, basis_z)
    return out.reshape(source.shape)


def solution(mesh):
    placed = (P("row", "col", None), P(), P(), P(), P(), P(), P())
    return jax.shard_map(
        local, mesh=mesh, in_specs=placed, out_specs=P("row", "col", None), check_vma=False
    )
```

time: 292 us -> 156 us (0.53); the launches traced: 286 us -> 156 us
  matrix products: 87.7 us -> 0 us
  local copies, waits for them, and re-layouts: 49.4 us -> 1.24 us
  Pallas kernels: 0 us -> 38.1 us
  other arithmetic: 27.8 us -> 0 us
  waiting for transfers between devices: 50.6 us -> 46.5 us
    dot_general x6 -> x0, matrix products: 87.7 us -> none  [the longest x1 32.7 us: local(): field = jnp.einsum('ck,abk->abc', basis_z, field[0], precision=HIGH)]
    pallas_call x0 -> x4, Pallas kernels: none -> 38.1 us  [the longest x1 19.6 us: local(): pl.pallas_call(planes, out_shape=jax.ShapeDtypeStruct(shape, F32), grid=(...]
    unnamed x16 -> x0, local copies, waits for them, and re-layouts: 34.7 us -> none
    all_to_all x2 -> x0, other arithmetic: 27.7 us -> none  [the longest x1 13.8 us: local(): lax.all_to_all(field, ('row', 'col'), split_axis=0, concat_axis=3, tiled=...]
    broadcast_in_dim x1 -> x0, local copies, waits for them, and re-layouts: 9.12 us -> none  [local(): field = field[None]]
    transpose x1 -> x0, local copies, waits for them, and re-layouts: 4.25 us -> none  [local(): field = jnp.einsum('rai,icbk->rcabk', blocks_x, field, precision=HIGH)]
    all_to_all x1, waiting for transfers between devices: 50.6 us -> 46.5 us  [local(): field = lax.all_to_all(sent, AXES, split_axis=0, concat_axis=0, tiled=True)]
  transfers between devices with their start and end apart: 1 -> 1, of which waited for: 1 -> 1; matrix products, arithmetic and copies ran while one was open for 0% -> 1% of each run, Pallas kernels for 0% -> 3%
where the time goes in v1:
time: 156 us
  blocking collectives  58.2 us (37%)
  waiting for transfers between devices  46.5 us (30%)
  Pallas kernels  38.1 us (24%)
  starting transfers between devices  11.9 us (8%)
    all_to_all x1, blocking collectives, local(): field = lax.all_to_all(field, AXES, split_axis=0, concat_axis=0, tiled=True)  58.2 us
    all_to_all x1, waiting for transfers between devices, local(): field = lax.all_to_all(sent, AXES, split_axis=0, concat_axis=0, tiled=True)  46.5 us
    pallas_call x1, Pallas kernels, local(): pl.pallas_call(planes, out_shape=jax.ShapeDtypeStruct(shape, F32), grid=(...  19.6 us
    all_to_all x1, starting transfers between devices, local(): field = lax.all_to_all(sent, AXES, split_axis=0, concat_axis=0, tiled=True)  11.9 us
    pallas_call x1, Pallas kernels, local(): pl.pallas_call(forward_z, out_shape=jax.ShapeDtypeStruct((devices, 64, 12...  7.4 us
    pallas_call x1, Pallas kernels, local(): pl.pallas_call(backward_z, out_shape=jax.ShapeDtypeStruct((lines, n), F32...  7.23 us
    pallas_call x1, Pallas kernels, local(): pl.pallas_call(prepare, out_shape=[jax.ShapeDtypeStruct(square, BF16)] *...  3.9 us
  transfers between devices with their start and end apart: 1, of which 1 were waited for; matrix products, arithmetic and copies ran while one was open for 1% of the time, Pallas kernels for 3%

profile of v1, /device:TPU:1, one launch (start us, length us, event | category | flops | bytes accessed | tf_op | source)
XLA Modules:
  0.0 155.9 jit_solution(692715384935688859)
XLA Ops:
  0.0 7.4 %forward_z.1 = f32[128,64,128]{2,1,0:T(8,128)} custom-call(f32[2048,512]{1,0:T(8,128)} %bitcast.7, f32[512,512]{1,0:T(8,128)} %basis_ref.3), custom_call_target="tpu_custom_call" | custom-call | tf_op jit(solution)/shard_map/forward_z/pallas_call | solution.py:133
  7.4 11.9 %all-to-all-start = ((f32[128,64,128]{2,1,0:T(8,128)}), f32[128,64,128]{2,1,0:T(8,128)}, u32[]{:S(2)}, u32[]{:S(2)}) async-start(f32[128,64,128]{2,1,0:T(8,128)} %forward_z.1), calls=%async_computation | async-start | bytes 8388608 | tf_op jit(solution)/shard_map/all_to_all | solution.py:143
  19.4 1.2 dynamic_slice.3.part_z
  20.6 3.9 %prepare.1 = (bf16[512,512]{1,0:T(8,128)(2,1)}, bf16[512,512]{1,0:T(8,128)(2,1)}, bf16[512,512]{1,0:T(8,128)(2,1)}, bf16[512,512]{1,0:T(8,128)(2,1)}, bf16[512,5...) custom-call(f32[512,512]{1,0:T(8,128)} %basis_x.1, ...), custom_call_target="tpu_custom_call" | custom-call | tf_op jit(solution)/shard_map/prepare/pallas_call | solution.py:145
  24.5 46.5 %all-to-all-done = f32[128,64,128]{2,1,0:T(8,128)} async-done(((f32[128,64,128]{2,1,0:T(8,128)}), f32[128,64,128]{2,1,0:T(8,128)}, u32[]{:S(2)}, u32[]{:S(2)}) %all-to-all-start) | async-done | bytes 4194336 | tf_op jit(solution)/shard_map/all_to_all | solution.py:143
  71.0 19.6 %planes.1 = f32[16,8,2,4,8,128]{5,4,3,2,1,0:T(8,128)} custom-call(f32[16,8,2,4,8,128]{5,4,3,2,1,0:T(8,128)} %bitcast.1.field_ref, bf16[512,512]{1,0:T(8,128)(2,1)} %get-tuple-element.14.xt_high, bf16[512,512]{1,0:T(8,128)(2,1)} %get-tuple-element.15.xt_low, bf16[512,512]{1,0:T(8,128)(2,1)} %get-tuple-element.16.x_high, ...), custom_call_target="tpu_custom_call" | custom-call | tf_op jit(solution)/shard_map/planes/pallas_call | solution.py:155
  90.5 58.2 %all_to_all.10.field_ref = f32[128,64,128]{2,1,0:T(8,128)} all-to-all(f32[128,64,128]{2,1,0:T(8,128)} %bitcast.6), channel_id=1, replica_groups=mesh['row'=16,'col'=8] {'row','col'}, dimensions={0} | all-to-all | bytes 8388608 | tf_op jit(solution)/shard_map/all_to_all | solution.py:169
  148.7 7.2 %backward_z.1 = f32[2048,512]{1,0:T(8,128)} custom-call(f32[128,64,128]{2,1,0:T(8,128)} %all_to_all.10.field_ref, f32[512,512]{1,0:T(8,128)} %basis_ref.3), custom_call_target="tpu_custom_call" | custom-call | tf_op jit(solution)/shard_map/backward_z/pallas_call | solution.py:170
Async XLA Ops:
  7.4 63.6 %all-to-all-start = ((f32[128,64,128]{2,1,0:T(8,128)}), f32[128,64,128]{2,1,0:T(8,128)}, u32[]{:S(2)}, u32[]{:S(2)}) async-start(f32[128,64,128]{2,1,0:T(8,128)} %forward_z.1), calls=%async_computation | async-start | bytes 8388608 | tf_op jit(solution)/shard_map/all_to_all | solution.py:143

commit v2 on v1

v2 whole, which is shorter than its diff:
```python
import jax
import jax.numpy as jnp
from jax import lax
from jax.experimental import pallas as pl
from jax.experimental.pallas import tpu as pltpu
from jax.sharding import PartitionSpec as P

F32 = jnp.float32
BF16 = jnp.bfloat16
AXES = ("row", "col")
NT = (((1,), (1,)), ((), ()))
NN = (((1,), (0,)), ((), ()))
MIB = 1 << 20


def halves(value):
    high = value.astype(BF16)
    low = (value - high.astype(F32)).astype(BF16)
    return high, low


def product(left, right, dims=NN):
    return lax.dot_general(left, right, dims, preferred_element_type=F32)


def product3(left, right, dims=NN):
    left_high, left_low = left
    right_high, right_low = right
    return (
        product(left_high, right_high, dims)
        + product(left_high, right_low, dims)
        + product(left_low, right_high, dims)
    )


def forward_z(
    source_hbm, basis_hbm, out_hbm, high_hbm, low_hbm,
    source_ref, basis_ref, out_ref, high_ref, low_ref, sems,
):
    n_z = basis_ref.shape[0]
    parts = source_ref.shape[0] // 512
    reads = [pltpu.make_async_copy(basis_hbm, basis_ref, sems.at[parts])]
    for part in range(parts):
        at = pl.ds(part * 512, 512)
        reads.append(pltpu.make_async_copy(source_hbm.at[at], source_ref.at[at], sems.at[part]))
    for read in reads:
        read.start()
    reads[0].wait()
    high_ref[...], low_ref[...] = halves(basis_ref[...].T)
    writes = [
        pltpu.make_async_copy(high_ref, high_hbm, sems.at[parts + 1]),
        pltpu.make_async_copy(low_ref, low_hbm, sems.at[parts + 2]),
    ]
    for write in writes:
        write.start()
    flat = out_ref.reshape(n_z * 16, 128)
    for pair in range(2 * parts):
        if pair % 2 == 0:
            reads[1 + pair // 2].wait()
        lines = halves(source_ref[pl.ds(pair * 256, 256), :])
        result = product3((high_ref[...], low_ref[...]), lines, NT)
        flat[pl.ds(2 * pair, n_z, stride=16), :] = result[:, :128]
        flat[pl.ds(2 * pair + 1, n_z, stride=16), :] = result[:, 128:]
        if pair % 4 == 3:
            at = pl.ds(pair // 4 * 8, 8)
            writes.append(
                pltpu.make_async_copy(
                    out_ref.at[:, :, at], out_hbm.at[:, :, at], sems.at[parts + 3 + pair // 4]
                )
            )
            writes[-1].start()
    for write in writes:
        write.wait()


def backward_z(field_ref, high_ref, low_ref, out_hbm, out_ref, sems):
    n_z = high_ref.shape[0]
    flat = field_ref.reshape(n_z * 16, 128)
    copies = []
    for part in range(out_ref.shape[0] // 512):
        for pair in range(2):
            first = part * 4 + pair * 2
            lines = jnp.concatenate(
                [flat[pl.ds(first + side, n_z, stride=16), :].T for side in range(2)], axis=0
            )
            out_ref[pl.ds(first * 128, 256), :] = product3(
                halves(lines), (high_ref[...], low_ref[...])
            )
        at = pl.ds(part * 512, 512)
        copies.append(pltpu.make_async_copy(out_ref.at[at], out_hbm.at[at], sems.at[part]))
        copies[-1].start()
    for copy in copies:
        copy.wait()


def prepare(
    basis_x, basis_y, eigen_x,
    xt_high, xt_low, x_high, x_low, y_high, y_low, yt_high, yt_low, column, strips,
):
    half = basis_x.shape[0] // 2
    for strip in range(strips.shape[0]):
        strips[strip] = basis_x[:, pl.ds(strip * 128, 128)]
    ordered = jnp.concatenate(
        [
            jnp.concatenate(
                [strips[strip, pl.ds(side, half, stride=2), :] for strip in range(strips.shape[0])],
                axis=1,
            )
            for side in range(2)
        ],
        axis=0,
    )
    x_high[...], x_low[...] = halves(ordered)
    xt_high[...], xt_low[...] = halves(ordered.T)
    y_high[...], y_low[...] = halves(basis_y[...])
    yt_high[...], yt_low[...] = halves(basis_y[...].T)
    column[...] = jnp.broadcast_to(eigen_x[...], (128, eigen_x.shape[1])).T


def planes(
    field_hbm, xt_high_hbm, xt_low_hbm, x_high_hbm, x_low_hbm,
    y_high_hbm, y_low_hbm, yt_high_hbm, yt_low_hbm, column_hbm, eigen_y, part_z, out_ref,
    field_ref, xt_high, xt_low, x_high, x_low, y_high, y_low, yt_high, yt_low, column,
    plane_high, plane_low, sems,
):
    count, rows_n, cols_n = field_ref.shape[:3]
    half = rows_n * 16
    first = lax.broadcasted_iota(jnp.int32, (half, 128), 1) < 64

    def read_plane(plane):
        return pltpu.make_async_copy(field_hbm.at[:, :, plane], field_ref.at[plane], sems.at[plane])

    tables = [
        pltpu.make_async_copy(source, target, sems.at[count + at])
        for at, (source, target) in enumerate(
            (
                (xt_high_hbm, xt_high), (xt_low_hbm, xt_low), (y_high_hbm, y_high),
                (y_low_hbm, y_low), (column_hbm, column), (yt_high_hbm, yt_high),
                (yt_low_hbm, yt_low), (x_high_hbm, x_high), (x_low_hbm, x_low),
            )
        )
    ]
    read_plane(0).start()
    tables[0].start()
    tables[1].start()
    read_plane(1).start()
    for table in tables[2:]:
        table.start()
    for plane in range(2, count):
        read_plane(plane).start()

    def gather(plane, side):
        read_plane(plane).wait()
        for pair in range(cols_n // 2):
            left = field_ref[plane, :, 2 * pair].reshape(half, 128)
            right = field_ref[plane, :, 2 * pair + 1].reshape(half, 128)
            even = jnp.where(first, left, pltpu.roll(right, 64, 1))
            odd = jnp.where(first, pltpu.roll(left, 64, 1), right)
            at = pl.ds(pair * 128, 128)
            for rows, value in ((pl.ds(0, half), even), (pl.ds(half, half), odd)):
                plane_high[side, rows, at], plane_low[side, rows, at] = halves(value)

    def scatter(plane, field):
        for pair in range(cols_n // 2):
            even = field[:half, pair * 128 : pair * 128 + 128]
            odd = field[half:, pair * 128 : pair * 128 + 128]
            left = jnp.where(first, even, pltpu.roll(odd, 64, 1))
            right = jnp.where(first, pltpu.roll(even, 64, 1), odd)
            out_ref[:, 2 * pair, plane] = left.reshape(rows_n, 16, 128)
            out_ref[:, 2 * pair + 1, plane] = right.reshape(rows_n, 16, 128)

    tables[0].wait()
    tables[1].wait()

    @pl.loop(0, count // 2)
    def _(step):
        sides = range(2)
        fields = [None, None]
        gather(2 * step, 0)
        for side in sides:
            if side == 0:
                gather(2 * step + 1, 1)
            fields[side] = product3(
                (xt_high[...], xt_low[...]), (plane_high[side], plane_low[side])
            )

        @pl.when(step == 0)
        def _():
            for table in tables[2:]:
                table.wait()

        for side in sides:
            fields[side] = product3(halves(fields[side]), (y_high[...], y_low[...]))
        for side in sides:
            denom = column[:, :1] + (eigen_y[...] + part_z[2 * step + side])
            fields[side] = product3(halves(fields[side] / denom), (yt_high[...], yt_low[...]))
        for side in sides:
            fields[side] = product3((x_high[...], x_low[...]), halves(fields[side]))
            scatter(2 * step + side, fields[side])


VMEM_SPEC = pl.BlockSpec(memory_space=pltpu.VMEM)
HBM_SPEC = pl.BlockSpec(memory_space=pltpu.HBM)


def limit(mebibytes):
    return pltpu.CompilerParams(vmem_limit_bytes=mebibytes * MIB)


def local(source, basis_x, basis_y, basis_z, eigen_x, eigen_y, eigen_z):
    rows_n, cols_n = lax.axis_size("row"), lax.axis_size("col")
    devices = rows_n * cols_n
    n = basis_z.shape[0]
    square = (n, n)
    lines = source.shape[0] * source.shape[1]
    table = jax.ShapeDtypeStruct(square, BF16)

    sent, z_high, z_low = pl.pallas_call(
        forward_z,
        out_shape=[jax.ShapeDtypeStruct((devices, 4, 16, 128), F32), table, table],
        in_specs=[HBM_SPEC] * 2,
        out_specs=[HBM_SPEC] * 3,
        scratch_shapes=[
            pltpu.VMEM((lines, n), F32),
            pltpu.VMEM(square, F32),
            pltpu.VMEM((devices, 4, 16, 128), F32),
            pltpu.VMEM(square, BF16),
            pltpu.VMEM(square, BF16),
            pltpu.SemaphoreType.DMA((lines // 512 + 5,)),
        ],
        name="forward_z",
    )(source.reshape(lines, n), basis_z)
    sent = sent.reshape(devices, 64, 128)
    field = lax.all_to_all(sent, AXES, split_axis=0, concat_axis=0, tiled=True)

    tables = pl.pallas_call(
        prepare,
        out_shape=[table] * 8 + [jax.ShapeDtypeStruct((n, 128), F32)],
        scratch_shapes=[pltpu.VMEM((n // 128, n, 128), F32)],
        name="prepare",
    )(basis_x, basis_y, eigen_x.reshape(1, n))
    device = lax.axis_index("row") * cols_n + lax.axis_index("col")
    part_z = lax.dynamic_slice_in_dim(eigen_z, device * 4, 4, 0)
    shape = (rows_n, cols_n, 4, 16, 128)
    field = pl.pallas_call(
        planes,
        out_shape=jax.ShapeDtypeStruct(shape, F32),
        in_specs=[HBM_SPEC] * 10 + [VMEM_SPEC, pl.BlockSpec(memory_space=pltpu.SMEM)],
        out_specs=VMEM_SPEC,
        scratch_shapes=[pltpu.VMEM((4, rows_n, cols_n, 16, 128), F32)]
        + [pltpu.VMEM(square, BF16)] * 8
        + [pltpu.VMEM((n, 128), F32)]
        + [pltpu.VMEM((2,) + square, BF16)] * 2
        + [pltpu.SemaphoreType.DMA((13,))],
        compiler_params=limit(40),
        name="planes",
    )(*[pltpu.with_memory_space_constraint(a, pltpu.HBM) for a in (field.reshape(shape), *tables)], eigen_y.reshape(1, n), part_z)

    field = field.reshape(devices, 64, 128)
    field = lax.all_to_all(field, AXES, split_axis=0, concat_axis=0, tiled=True)
    out = pl.pallas_call(
        backward_z,
        out_shape=jax.ShapeDtypeStruct((lines, n), F32),
        in_specs=[VMEM_SPEC] * 3,
        out_specs=HBM_SPEC,
        scratch_shapes=[
            pltpu.VMEM((lines, n), F32), pltpu.SemaphoreType.DMA((lines // 512,))
        ],
        compiler_params=limit(20),
        name="backward_z",
    )(field, z_high, z_low)
    return out.reshape(source.shape)


def solution(mesh):
    placed = (P("row", "col", None), P(), P(), P(), P(), P(), P())
    return jax.shard_map(
        local, mesh=mesh, in_specs=placed, out_specs=P("row", "col", None), check_vma=False
    )
```

time: 156 us -> 152 us (0.974)
  Pallas kernels: 38.1 us -> 34.4 us
    pallas_call x3, Pallas kernels: 30.9 us -> 28.9 us  [the longest x1 17.1 us: local(): pl.pallas_call(planes, out_shape=jax.ShapeDtypeStruct(shape, F32), in_spe...]
    pallas_call x1, Pallas kernels: 7.23 us -> 5.56 us  [local(): pl.pallas_call(backward_z, out_shape=jax.ShapeDtypeStruct((lines, n), F32...]
  transfers between devices with their start and end apart: 1 -> 1, of which waited for: 1 -> 1; matrix products, arithmetic and copies ran while one was open for 1% -> 0% of each run, Pallas kernels for 3% -> 3%
where the time goes in v2:
time: 152 us
  blocking collectives  57.9 us (38%)
  waiting for transfers between devices  46.9 us (31%)
  Pallas kernels  34.4 us (23%)
  starting transfers between devices  11.9 us (8%)
    all_to_all x1, blocking collectives, local(): field = lax.all_to_all(field, AXES, split_axis=0, concat_axis=0, tiled=True)  57.9 us
    all_to_all x1, waiting for transfers between devices, local(): field = lax.all_to_all(sent, AXES, split_axis=0, concat_axis=0, tiled=True)  46.9 us
    pallas_call x1, Pallas kernels, local(): pl.pallas_call(planes, out_shape=jax.ShapeDtypeStruct(shape, F32), in_spe...  17.1 us
    all_to_all x1, starting transfers between devices, local(): field = lax.all_to_all(sent, AXES, split_axis=0, concat_axis=0, tiled=True)  11.9 us
    pallas_call x1, Pallas kernels, local(): pl.pallas_call(forward_z, out_shape=[jax.ShapeDtypeStruct((devices, 4, 16...  7.85 us
    pallas_call x1, Pallas kernels, local(): pl.pallas_call(backward_z, out_shape=jax.ShapeDtypeStruct((lines, n), F32...  5.56 us
    pallas_call x1, Pallas kernels, local(): pl.pallas_call(prepare, out_shape=[table] * 8 + [jax.ShapeDtypeStruct((n,...  3.96 us
  transfers between devices with their start and end apart: 1, of which 1 were waited for; matrix products, arithmetic and copies ran while one was open for 0% of the time, Pallas kernels for 3%

profile of v2, /device:TPU:1, one launch (start us, length us, event | category | flops | bytes accessed | tf_op | source)
XLA Modules:
  0.0 152.2 jit_solution(14120821377459731047)
XLA Ops:
  0.0 7.9 %forward_z.1 = (f32[128,4,16,128]{3,2,1,0:T(8,128)}, bf16[512,512]{1,0:T(8,128)(2,1)}, bf16[512,512]{1,0:T(8,128)(2,1)}) custom-call(f32[2048,512]{1,0:T(8,128)} %bitcast.9, f32[512,512]{1,0:T(8,128)} %basis_hbm.1), custom_call_target="tpu_custom_call" | custom-call | tf_op jit(solution)/shard_map/forward_z/pallas_call | solution.py:218
  7.9 0.0 copy-start.2
  7.9 11.9 %all-to-all-start = ((f32[128,64,128]{2,1,0:T(8,128)}), f32[128,64,128]{2,1,0:T(8,128)}, u32[]{:S(2)}, u32[]{:S(2)}) async-start(f32[128,64,128]{2,1,0:T(8,128)} %bitcast.10), calls=%async_computation | async-start | bytes 8388608 | tf_op jit(solution)/shard_map/all_to_all | solution.py:234
  19.8 0.8 dynamic_slice.3.part_z
  20.6 4.0 %prepare.1 = (bf16[512,512]{1,0:T(8,128)(2,1)}, bf16[512,512]{1,0:T(8,128)(2,1)}, bf16[512,512]{1,0:T(8,128)(2,1)}, bf16[512,512]{1,0:T(8,128)(2,1)}, bf16[512,5...) custom-call(f32[512,512]{1,0:T(8,128)} %basis_x.1, ...), custom_call_target="tpu_custom_call" | custom-call | tf_op jit(solution)/shard_map/prepare/pallas_call | solution.py:236
  24.6 46.9 %all-to-all-done = f32[128,64,128]{2,1,0:T(8,128)} async-done(((f32[128,64,128]{2,1,0:T(8,128)}), f32[128,64,128]{2,1,0:T(8,128)}, u32[]{:S(2)}, u32[]{:S(2)}) %all-to-all-start) | async-done | bytes 4194336 | tf_op jit(solution)/shard_map/all_to_all | solution.py:234
  71.4 0.0 copy-done.2
  71.5 17.1 %planes.1 = f32[16,8,4,16,128]{4,3,2,1,0:T(8,128)S(1)} custom-call(f32[16,8,4,16,128]{4,3,2,1,0:T(8,128)} %bitcast.2.field_hbm, bf16[512,512]{1,0:T(8,128)(2,1)} %get-tuple-element.18.xt_high_hbm, bf16[512,512]{1,0:T(8,128)(2,1)} %get-tuple-element.19.xt_low_hbm, bf16[512,512]{1,0:T(8,128)(2,1)} %get-tuple-element.20.x_high_hbm, ...), custom_call_target="tpu_custom_call" | custom-call | tf_op jit(solution)/shard_map/planes/pallas_call | solution.py:245
  88.5 0.0 copy-start
  88.5 0.0 copy-start.1
  88.6 57.9 %all_to_all.10.field_ref = f32[128,64,128]{2,1,0:T(8,128)S(1)} all-to-all(f32[128,64,128]{2,1,0:T(8,128)S(1)} %bitcast.7), channel_id=1, replica_groups=mesh['row'=16,'col'=8] {'row','col'}, dimensions={0} | all-to-all | bytes 8388608 | tf_op jit(solution)/shard_map/all_to_all | solution.py:260
  146.4 0.0 copy-done
  146.4 0.0 copy-done.1
  146.4 5.6 %backward_z.1 = f32[2048,512]{1,0:T(8,128)} custom-call(f32[128,64,128]{2,1,0:T(8,128)S(1)} %all_to_all.10.field_ref, bf16[512,512]{1,0:T(8,128)(2,1)S(1)} %copy-done, bf16[512,512]{1,0:T(8,128)(2,1)S(1)} %copy-done.1), custom_call_target="tpu_custom_call" | custom-call | tf_op jit(solution)/shard_map/backward_z/pallas_call | solution.py:261
Async XLA Ops:
  7.9 63.6 %copy-start.2 = (f32[512]{0:T(512)S(1)}, f32[512]{0:T(512)}, u32[]{:S(2)}) copy-start(f32[512]{0:T(512)} %param.12) | copy-start | bytes 6148
  7.9 63.6 %all-to-all-start = ((f32[128,64,128]{2,1,0:T(8,128)}), f32[128,64,128]{2,1,0:T(8,128)}, u32[]{:S(2)}, u32[]{:S(2)}) async-start(f32[128,64,128]{2,1,0:T(8,128)} %bitcast.10), calls=%async_computation | async-start | bytes 8388608 | tf_op jit(solution)/shard_map/all_to_all | solution.py:234
  88.5 57.9 %copy-start = (bf16[512,512]{1,0:T(8,128)(2,1)S(1)}, bf16[512,512]{1,0:T(8,128)(2,1)}, u32[]{:S(2)}) copy-start(bf16[512,512]{1,0:T(8,128)(2,1)} %get-tuple-element.27.high_ref) | copy-start | bytes 1572868
  88.5 57.9 %copy-start.1 = (bf16[512,512]{1,0:T(8,128)(2,1)S(1)}, bf16[512,512]{1,0:T(8,128)(2,1)}, u32[]{:S(2)}) copy-start(bf16[512,512]{1,0:T(8,128)(2,1)} %get-tuple-element.28.low_ref) | copy-start | bytes 1572868

commit v3 on v2

v3 whole, which is shorter than its diff:
```python
import jax
import jax.numpy as jnp
from jax import lax
from jax.experimental import pallas as pl
from jax.experimental.pallas import tpu as pltpu
from jax.sharding import PartitionSpec as P

F32 = jnp.float32
BF16 = jnp.bfloat16
AXES = ("row", "col")
NT = (((1,), (1,)), ((), ()))
NN = (((1,), (0,)), ((), ()))
MIB = 1 << 20


def halves(value):
    high = value.astype(BF16)
    low = (value - high.astype(F32)).astype(BF16)
    return high, low


def product(left, right, dims=NN):
    return lax.dot_general(left, right, dims, preferred_element_type=F32)


def product3(left, right, dims=NN):
    left_high, left_low = left
    right_high, right_low = right
    return (
        product(left_high, right_high, dims)
        + product(left_high, right_low, dims)
        + product(left_low, right_high, dims)
    )


def forward_z(
    source_hbm, basis_hbm, out_hbm, both_hbm, source_ref, basis_ref, out_ref, both_ref, sems,
):
    n_z = basis_ref.shape[0]
    parts = source_ref.shape[0] // 512
    reads = [pltpu.make_async_copy(basis_hbm, basis_ref, sems.at[parts])]
    for part in range(parts):
        at = pl.ds(part * 512, 512)
        reads.append(pltpu.make_async_copy(source_hbm.at[at], source_ref.at[at], sems.at[part]))
    for read in reads:
        read.start()
    reads[0].wait()
    both_ref[pl.ds(0, n_z), :], both_ref[pl.ds(n_z, n_z), :] = halves(basis_ref[...].T)
    writes = [pltpu.make_async_copy(both_ref, both_hbm, sems.at[parts + 1])]
    writes[0].start()
    flat = out_ref.reshape(2 * n_z * 8, 128)
    for pair in range(2 * parts):
        if pair % 4 == 0:
            reads[1 + pair // 2].wait()
            reads[2 + pair // 2].wait()
        high, low = halves(source_ref[pl.ds(pair * 256, 256), :])
        result = product(both_ref[...], high, NT)
        result = result[:n_z] + result[n_z:] + product(both_ref[pl.ds(0, n_z), :], low, NT)
        half = pair // 4
        for side in range(2):
            at = half * n_z * 8 + pair % 4 * 2 + side
            flat[pl.ds(at, n_z, stride=8), :] = result[:, side * 128 : side * 128 + 128]
        if pair % 4 == 3:
            writes.append(
                pltpu.make_async_copy(
                    out_ref.at[half], out_hbm.at[:, half], sems.at[parts + 2 + half]
                )
            )
            writes[-1].start()
    for write in writes:
        write.wait()


def backward_z(field_ref, both_ref, out_hbm, tiles_ref, out_ref, sems):
    n_z = both_ref.shape[0] // 2
    table = both_ref[pl.ds(0, n_z), :], both_ref[pl.ds(n_z, n_z), :]
    writes = []
    for half in range(2):
        tiles_ref[half] = field_ref[:, :, pl.ds(half * 8, 8), :].reshape(n_z * 8, 128)
        for pair in range(4):
            lines = jnp.concatenate(
                [
                    tiles_ref[half, pl.ds(pair * 2 + side, n_z, stride=8), :].T
                    for side in range(2)
                ],
                axis=0,
            )
            at = pl.ds((half * 4 + pair) * 256, 256)
            out_ref[at, :] = product3(halves(lines), table)
            writes.append(
                pltpu.make_async_copy(out_ref.at[at], out_hbm.at[at], sems.at[half * 4 + pair])
            )
            writes[-1].start()
    for write in writes:
        write.wait()


def prepare(
    basis_x, basis_y, eigen_x,
    xt_high, xt_low, x_high, x_low, y_high, y_low, yt_high, yt_low, column, strips,
):
    half = basis_x.shape[0] // 2
    for strip in range(strips.shape[0]):
        strips[strip] = basis_x[:, pl.ds(strip * 128, 128)]
    ordered = jnp.concatenate(
        [
            jnp.concatenate(
                [strips[strip, pl.ds(side, half, stride=2), :] for strip in range(strips.shape[0])],
                axis=1,
            )
            for side in range(2)
        ],
        axis=0,
    )
    x_high[...], x_low[...] = halves(ordered)
    xt_high[...], xt_low[...] = halves(ordered.T)
    y_high[...], y_low[...] = halves(basis_y[...])
    yt_high[...], yt_low[...] = halves(basis_y[...].T)
    column[...] = jnp.broadcast_to(eigen_x[...], (128, eigen_x.shape[1])).T


def planes(
    field_hbm, xt_high_hbm, xt_low_hbm, x_high_hbm, x_low_hbm,
    y_high_hbm, y_low_hbm, yt_high_hbm, yt_low_hbm, column_hbm, eigen_y, eigen_z, out_ref,
    field_ref, xt_high, xt_low, x_high, x_low, y_high, y_low, yt_high, yt_low, column,
    plane_high, plane_low, sems,
):
    count, rows_n, cols_n = field_ref.shape[:3]
    owned = (lax.axis_index("row") * cols_n + lax.axis_index("col")) * count
    half = rows_n * 16
    lower = lax.broadcasted_iota(jnp.int32, (half, 128), 1) < 64

    def read_plane(plane):
        return pltpu.make_async_copy(field_hbm.at[:, :, :, plane], field_ref.at[plane], sems.at[plane])

    tables = [
        pltpu.make_async_copy(source, target, sems.at[count + at])
        for at, (source, target) in enumerate(
            (
                (xt_high_hbm, xt_high), (xt_low_hbm, xt_low), (y_high_hbm, y_high),
                (y_low_hbm, y_low), (column_hbm, column), (yt_high_hbm, yt_high),
                (yt_low_hbm, yt_low), (x_high_hbm, x_high), (x_low_hbm, x_low),
            )
        )
    ]
    read_plane(0).start()
    tables[0].start()
    tables[1].start()
    read_plane(1).start()
    for table in tables[2:]:
        table.start()
    for plane in range(2, count):
        read_plane(plane).start()

    def gather(plane, side):
        for pair in range(cols_n // 2):
            left = field_ref[plane, :, 2 * pair].reshape(half, 128)
            right = field_ref[plane, :, 2 * pair + 1].reshape(half, 128)
            even = jnp.where(lower, left, pltpu.roll(right, 64, 1))
            odd = jnp.where(lower, pltpu.roll(left, 64, 1), right)
            at = pl.ds(pair * 128, 128)
            for rows, value in ((pl.ds(0, half), even), (pl.ds(half, half), odd)):
                plane_high[side, rows, at], plane_low[side, rows, at] = halves(value)

    def scatter(plane, field):
        for pair in range(cols_n // 2):
            even = field[:half, pair * 128 : pair * 128 + 128]
            odd = field[half:, pair * 128 : pair * 128 + 128]
            left = jnp.where(lower, even, pltpu.roll(odd, 64, 1))
            right = jnp.where(lower, pltpu.roll(even, 64, 1), odd)
            out_ref[:, 2 * pair, plane] = left.reshape(rows_n, 16, 128)
            out_ref[:, 2 * pair + 1, plane] = right.reshape(rows_n, 16, 128)

    fields = [None] * count

    def into_x(plane):
        side = plane % 2
        fields[plane] = product3(
            (xt_high[...], xt_low[...]), (plane_high[side], plane_low[side])
        )

    def into_y(plane):
        fields[plane] = product3(halves(fields[plane]), (y_high[...], y_low[...]))

    def out_of_y(plane):
        denom = column[:, :1] + (eigen_y[...] + eigen_z[owned + plane])
        fields[plane] = product3(halves(fields[plane] / denom), (yt_high[...], yt_low[...]))

    def out_of_x(plane):
        fields[plane] = product3((x_high[...], x_low[...]), halves(fields[plane]))

    read_plane(0).wait()
    gather(0, 0)
    read_plane(1).wait()
    tables[0].wait()
    tables[1].wait()
    for first in range(0, count, 2):
        second = first + 1
        into_x(first)
        gather(second, 1)
        if first > 0:
            scatter(first - 1, fields[first - 1])
        into_x(second)
        if first == 0:
            for table in tables[2:]:
                table.wait()
            for plane in range(2, count):
                read_plane(plane).wait()
        for stage in (into_y, out_of_y):
            stage(first)
            stage(second)
        out_of_x(first)
        if second + 1 < count:
            gather(second + 1, 0)
        scatter(first, fields[first])
        out_of_x(second)
    scatter(count - 1, fields[count - 1])


VMEM_SPEC = pl.BlockSpec(memory_space=pltpu.VMEM)
HBM_SPEC = pl.BlockSpec(memory_space=pltpu.HBM)


def limit(mebibytes):
    return pltpu.CompilerParams(vmem_limit_bytes=mebibytes * MIB)


def local(source, basis_x, basis_y, basis_z, eigen_x, eigen_y, eigen_z):
    rows_n, cols_n = lax.axis_size("row"), lax.axis_size("col")
    devices = rows_n * cols_n
    n = basis_z.shape[0]
    square = (n, n)
    lines = source.shape[0] * source.shape[1]
    table = jax.ShapeDtypeStruct(square, BF16)

    both = jax.ShapeDtypeStruct((2 * n, n), BF16)
    sent, both_z = pl.pallas_call(
        forward_z,
        out_shape=[jax.ShapeDtypeStruct((devices, 2, 32, 128), F32), both],
        in_specs=[HBM_SPEC] * 2,
        out_specs=[HBM_SPEC] * 2,
        scratch_shapes=[
            pltpu.VMEM((lines, n), F32),
            pltpu.VMEM(square, F32),
            pltpu.VMEM((2, devices, 32, 128), F32),
            pltpu.VMEM((2 * n, n), BF16),
            pltpu.SemaphoreType.DMA((lines // 512 + 4,)),
        ],
        name="forward_z",
    )(source.reshape(lines, n), basis_z)
    sent = sent.reshape(devices, 64, 128)
    field = lax.all_to_all(sent, AXES, split_axis=0, concat_axis=0, tiled=True)

    tables = pl.pallas_call(
        prepare,
        out_shape=[table] * 8 + [jax.ShapeDtypeStruct((n, 128), F32)],
        scratch_shapes=[pltpu.VMEM((n // 128, n, 128), F32)],
        name="prepare",
    )(basis_x, basis_y, eigen_x.reshape(1, n))
    shape = (rows_n, cols_n, 4, 16, 128)
    arrived = field.reshape(rows_n, cols_n, 2, 4, 8, 128)
    field = pl.pallas_call(
        planes,
        out_shape=jax.ShapeDtypeStruct(shape, F32),
        in_specs=[HBM_SPEC] * 10 + [VMEM_SPEC, pl.BlockSpec(memory_space=pltpu.SMEM)],
        out_specs=VMEM_SPEC,
        scratch_shapes=[pltpu.VMEM((4, rows_n, cols_n, 2, 8, 128), F32)]
        + [pltpu.VMEM(square, BF16)] * 8
        + [pltpu.VMEM((n, 128), F32)]
        + [pltpu.VMEM((2,) + square, BF16)] * 2
        + [pltpu.SemaphoreType.DMA((13,))],
        compiler_params=limit(40),
        name="planes",
    )(*[pltpu.with_memory_space_constraint(a, pltpu.HBM) for a in (arrived, *tables)], eigen_y.reshape(1, n), eigen_z)

    field = field.reshape(devices, 64, 128)
    field = lax.all_to_all(field, AXES, split_axis=0, concat_axis=0, tiled=True)
    out = pl.pallas_call(
        backward_z,
        out_shape=jax.ShapeDtypeStruct((lines, n), F32),
        in_specs=[VMEM_SPEC] * 2,
        out_specs=HBM_SPEC,
        scratch_shapes=[
            pltpu.VMEM((2, lines * 2, 128), F32),
            pltpu.VMEM((lines, n), F32),
            pltpu.SemaphoreType.DMA((lines // 256,)),
        ],
        compiler_params=limit(20),
        name="backward_z",
    )(field.reshape(devices, 4, 16, 128), both_z)
    return out.reshape(source.shape)


def solution(mesh):
    placed = (P("row", "col", None), P(), P(), P(), P(), P(), P())
    return jax.shard_map(
        local, mesh=mesh, in_specs=placed, out_specs=P("row", "col", None), check_vma=False
    )
```

time: 152 us -> 150 us (0.987)
  Pallas kernels: 34.4 us -> 32.1 us
where the time goes in v3:
time: 150 us
  blocking collectives  57.9 us (39%)
  waiting for transfers between devices  47.6 us (32%)
  Pallas kernels  32.1 us (21%)
  starting transfers between devices  12 us (8%)
    all_to_all x1, blocking collectives, local(): field = lax.all_to_all(field, AXES, split_axis=0, concat_axis=0, tiled=True)  57.9 us
    all_to_all x1, waiting for transfers between devices, local(): field = lax.all_to_all(sent, AXES, split_axis=0, concat_axis=0, tiled=True)  47.6 us
    pallas_call x1, Pallas kernels, local(): pl.pallas_call(planes, out_shape=jax.ShapeDtypeStruct(shape, F32), in_spe...  16.3 us
    all_to_all x1, starting transfers between devices, local(): field = lax.all_to_all(sent, AXES, split_axis=0, concat_axis=0, tiled=True)  12 us
    pallas_call x1, Pallas kernels, local(): pl.pallas_call(forward_z, out_shape=[jax.ShapeDtypeStruct((devices, 2, 32...  7.14 us
    pallas_call x1, Pallas kernels, local(): pl.pallas_call(backward_z, out_shape=jax.ShapeDtypeStruct((lines, n), F32...  4.69 us
    pallas_call x1, Pallas kernels, local(): pl.pallas_call(prepare, out_shape=[table] * 8 + [jax.ShapeDtypeStruct((n,...  3.97 us
  transfers between devices with their start and end apart: 1, of which 1 were waited for; matrix products, arithmetic and copies ran while one was open for 0% of the time, Pallas kernels for 3%

profile of v3, /device:TPU:1, one launch (start us, length us, event | category | flops | bytes accessed | tf_op | source)
XLA Modules:
  0.0 149.8 jit_solution(1134312281937495337)
XLA Ops:
  0.0 7.1 %forward_z.1 = (f32[128,2,32,128]{3,2,1,0:T(8,128)}, bf16[1024,512]{1,0:T(8,128)(2,1)}) custom-call(f32[2048,512]{1,0:T(8,128)} %bitcast.11, f32[512,512]{1,0:T(8,128)} %basis_hbm.1), custom_call_target="tpu_custom_call" | custom-call | tf_op jit(solution)/shard_map/forward_z/pallas_call | solution.py:237
  7.2 0.0 copy-start.1
  7.2 0.0 copy-start.2
  7.2 12.0 %all-to-all-start = ((f32[128,64,128]{2,1,0:T(8,128)}), f32[128,64,128]{2,1,0:T(8,128)}, u32[]{:S(2)}, u32[]{:S(2)}) async-start(f32[128,64,128]{2,1,0:T(8,128)} %bitcast.12), calls=%async_computation | async-start | bytes 8388608 | tf_op jit(solution)/shard_map/all_to_all | solution.py:252
  19.1 4.0 %prepare.1 = (bf16[512,512]{1,0:T(8,128)(2,1)}, bf16[512,512]{1,0:T(8,128)(2,1)}, bf16[512,512]{1,0:T(8,128)(2,1)}, bf16[512,512]{1,0:T(8,128)(2,1)}, bf16[512,5...) custom-call(f32[512,512]{1,0:T(8,128)} %basis_x.1, ...), custom_call_target="tpu_custom_call" | custom-call | tf_op jit(solution)/shard_map/prepare/pallas_call | solution.py:254
  23.1 47.6 %all-to-all-done = f32[128,64,128]{2,1,0:T(8,128)} async-done(((f32[128,64,128]{2,1,0:T(8,128)}), f32[128,64,128]{2,1,0:T(8,128)}, u32[]{:S(2)}, u32[]{:S(2)}) %all-to-all-start) | async-done | bytes 4194336 | tf_op jit(solution)/shard_map/all_to_all | solution.py:252
  70.8 0.0 copy-done.1
  70.8 0.0 copy-done.2
  70.8 16.3 %planes.1 = f32[16,8,4,16,128]{4,3,2,1,0:T(8,128)S(1)} custom-call(f32[16,8,2,4,8,128]{5,4,3,2,1,0:T(8,128)} %bitcast.2.field_hbm, bf16[512,512]{1,0:T(8,128)(2,1)} %get-tuple-element.17.xt_high_hbm, bf16[512,512]{1,0:T(8,128)(2,1)} %get-tuple-element.18.xt_low_hbm, bf16[512,512]{1,0:T(8,128)(2,1)} %get-tuple-element.19.x_high_hbm, ...), custom_call_target="tpu_custom_call" | custom-call | tf_op jit(solution)/shard_map/planes/pallas_call | solution.py:262
  87.1 0.0 copy-start
  87.1 57.9 %all_to_all.10 = f32[128,64,128]{2,1,0:T(8,128)S(1)} all-to-all(f32[128,64,128]{2,1,0:T(8,128)S(1)} %bitcast.8), channel_id=1, replica_groups=mesh['row'=16,'col'=8] {'row','col'}, dimensions={0} | all-to-all | bytes 8388608 | tf_op jit(solution)/shard_map/all_to_all | solution.py:277
  145.0 0.0 copy-done
  145.0 4.7 %backward_z.1 = f32[2048,512]{1,0:T(8,128)} custom-call(f32[128,4,16,128]{3,2,1,0:T(8,128)S(1)} %bitcast.9, bf16[1024,512]{1,0:T(8,128)(2,1)S(1)} %copy-done), custom_call_target="tpu_custom_call" | custom-call | tf_op jit(solution)/shard_map/backward_z/pallas_call | solution.py:278
Async XLA Ops:
  7.2 63.6 %copy-start.1 = (f32[512]{0:T(512)S(1)}, f32[512]{0:T(512)}, u32[]{:S(2)}) copy-start(f32[512]{0:T(512)} %param.12) | copy-start | bytes 6148
  7.2 63.6 %copy-start.2 = (f32[512]{0:T(512)S(1)}, f32[512]{0:T(512)}, u32[]{:S(2)}) copy-start(f32[512]{0:T(512)} %eigen_z.1) | copy-start | bytes 6148
  7.2 63.6 %all-to-all-start = ((f32[128,64,128]{2,1,0:T(8,128)}), f32[128,64,128]{2,1,0:T(8,128)}, u32[]{:S(2)}, u32[]{:S(2)}) async-start(f32[128,64,128]{2,1,0:T(8,128)} %bitcast.12), calls=%async_computation | async-start | bytes 8388608 | tf_op jit(solution)/shard_map/all_to_all | solution.py:252
  87.1 57.9 %copy-start = (bf16[1024,512]{1,0:T(8,128)(2,1)S(1)}, bf16[1024,512]{1,0:T(8,128)(2,1)}, u32[]{:S(2)}) copy-start(bf16[1024,512]{1,0:T(8,128)(2,1)} %get-tuple-element.26.both_ref) | copy-start | bytes 3145732

commit v4 on v3

v4 whole, which is shorter than its diff:
```python
import jax
import jax.numpy as jnp
from jax import lax
from jax.experimental import pallas as pl
from jax.experimental.pallas import tpu as pltpu
from jax.sharding import PartitionSpec as P

F32 = jnp.float32
BF16 = jnp.bfloat16
AXES = ("row", "col")
NT = (((1,), (1,)), ((), ()))
NN = (((1,), (0,)), ((), ()))
MIB = 1 << 20


def halves(value):
    high = value.astype(BF16)
    low = (value - high.astype(F32)).astype(BF16)
    return high, low


def product(left, right, dims=NN):
    return lax.dot_general(left, right, dims, preferred_element_type=F32)


def product3(left, right, dims=NN):
    left_high, left_low = left
    right_high, right_low = right
    return (
        product(left_high, right_high, dims)
        + product(left_high, right_low, dims)
        + product(left_low, right_high, dims)
    )


def forward_z(source_hbm, basis_hbm, out_ref, both_ref, source_ref, basis_ref, tiles_ref, sems):
    n_z = basis_ref.shape[0]
    parts = source_ref.shape[0] // 512
    reads = [pltpu.make_async_copy(basis_hbm, basis_ref, sems.at[parts])]
    for part in range(parts):
        at = pl.ds(part * 512, 512)
        reads.append(pltpu.make_async_copy(source_hbm.at[at], source_ref.at[at], sems.at[part]))
    for read in reads:
        read.start()
    reads[0].wait()
    both_ref[pl.ds(0, n_z), :], both_ref[pl.ds(n_z, n_z), :] = halves(basis_ref[...].T)
    for pair in range(2 * parts):
        if pair % 4 == 0:
            reads[1 + pair // 2].wait()
            reads[2 + pair // 2].wait()
        high, low = halves(source_ref[pl.ds(pair * 256, 256), :])
        result = product(both_ref[...], high, NT)
        result = result[:n_z] + result[n_z:] + product(both_ref[pl.ds(0, n_z), :], low, NT)
        half = pair // 4
        for side in range(2):
            at = pl.ds(pair % 4 * 2 + side, n_z, stride=8)
            tiles_ref[half, at, :] = result[:, side * 128 : side * 128 + 128]
        if pair % 4 == 3:
            out_ref[:, half] = tiles_ref[half].reshape(out_ref.shape[0], 32, 128)


def backward_z(field_ref, both_ref, out_hbm, tiles_ref, out_ref, sems):
    n_z = both_ref.shape[0] // 2
    table = both_ref[pl.ds(0, n_z), :], both_ref[pl.ds(n_z, n_z), :]
    writes = []
    for half in range(2):
        tiles_ref[half] = field_ref[:, :, pl.ds(half * 8, 8), :].reshape(n_z * 8, 128)
        for pair in range(4):
            lines = jnp.concatenate(
                [
                    tiles_ref[half, pl.ds(pair * 2 + side, n_z, stride=8), :].T
                    for side in range(2)
                ],
                axis=0,
            )
            at = pl.ds((half * 4 + pair) * 256, 256)
            out_ref[at, :] = product3(halves(lines), table)
            writes.append(
                pltpu.make_async_copy(out_ref.at[at], out_hbm.at[at], sems.at[half * 4 + pair])
            )
            writes[-1].start()
    for write in writes:
        write.wait()


def planes(
    field_ref, basis_x, basis_y, eigen_x, eigen_y, eigen_z, out_ref,
    strips, xt_high, xt_low, x_high, x_low, y_high, y_low, yt_high, yt_low, column,
    plane_high, plane_low,
):
    rows_n, cols_n, _, count = field_ref.shape[:4]
    n = basis_x.shape[0]
    half = rows_n * 16
    owned = (lax.axis_index("row") * cols_n + lax.axis_index("col")) * count
    lower = lax.broadcasted_iota(jnp.int32, (half, 128), 1) < 64

    def ordered(strip):
        return jnp.concatenate(
            [strips[strip, pl.ds(side, n // 2, stride=2), :] for side in range(2)], axis=0
        )

    def tables_xt():
        for strip in range(n // 128):
            at = pl.ds(strip * 128, 128)
            strips[strip] = basis_x[:, at]
            xt_high[at, :], xt_low[at, :] = halves(ordered(strip).T)

    def tables_x():
        for strip in range(n // 128):
            at = pl.ds(strip * 128, 128)
            x_high[:, at], x_low[:, at] = halves(ordered(strip))

    def tables_y():
        y_high[...], y_low[...] = halves(basis_y[...])
        column[...] = jnp.broadcast_to(eigen_x[...], (128, n)).T

    def tables_yt():
        yt_high[...], yt_low[...] = halves(basis_y[...].T)

    def gather(plane, side):
        for pair in range(cols_n // 2):
            left = field_ref[:, 2 * pair, :, plane].reshape(half, 128)
            right = field_ref[:, 2 * pair + 1, :, plane].reshape(half, 128)
            even = jnp.where(lower, left, pltpu.roll(right, 64, 1))
            odd = jnp.where(lower, pltpu.roll(left, 64, 1), right)
            at = pl.ds(pair * 128, 128)
            for rows, value in ((pl.ds(0, half), even), (pl.ds(half, half), odd)):
                plane_high[side, rows, at], plane_low[side, rows, at] = halves(value)

    def scatter(plane, field):
        for pair in range(cols_n // 2):
            even = field[:half, pair * 128 : pair * 128 + 128]
            odd = field[half:, pair * 128 : pair * 128 + 128]
            left = jnp.where(lower, even, pltpu.roll(odd, 64, 1))
            right = jnp.where(lower, pltpu.roll(even, 64, 1), odd)
            out_ref[:, 2 * pair, plane] = left.reshape(rows_n, 16, 128)
            out_ref[:, 2 * pair + 1, plane] = right.reshape(rows_n, 16, 128)

    fields = [None] * count

    def into_x(plane):
        side = plane % 2
        fields[plane] = product3(
            (xt_high[...], xt_low[...]), (plane_high[side], plane_low[side])
        )

    def into_y(plane):
        fields[plane] = product3(halves(fields[plane]), (y_high[...], y_low[...]))

    def out_of_y(plane):
        denom = column[:, :1] + (eigen_y[...] + eigen_z[owned + plane])
        fields[plane] = product3(halves(fields[plane] / denom), (yt_high[...], yt_low[...]))

    def out_of_x(plane):
        fields[plane] = product3((x_high[...], x_low[...]), halves(fields[plane]))

    tables_xt()
    gather(0, 0)
    for first in range(0, count, 2):
        second = first + 1
        into_x(first)
        gather(second, 1)
        if first == 0:
            tables_y()
        else:
            scatter(first - 1, fields[first - 1])
        into_x(second)
        if first == 0:
            tables_yt()
            tables_x()
        for stage in (into_y, out_of_y):
            stage(first)
            stage(second)
        out_of_x(first)
        if second + 1 < count:
            gather(second + 1, 0)
        scatter(first, fields[first])
        out_of_x(second)
    scatter(count - 1, fields[count - 1])


VMEM_SPEC = pl.BlockSpec(memory_space=pltpu.VMEM)
HBM_SPEC = pl.BlockSpec(memory_space=pltpu.HBM)


def in_hbm(value):
    return pltpu.with_memory_space_constraint(value, pltpu.HBM)


def limit(mebibytes):
    return pltpu.CompilerParams(vmem_limit_bytes=mebibytes * MIB)


def local(source, basis_x, basis_y, basis_z, eigen_x, eigen_y, eigen_z):
    rows_n, cols_n = lax.axis_size("row"), lax.axis_size("col")
    devices = rows_n * cols_n
    n = basis_z.shape[0]
    square = (n, n)
    lines = source.shape[0] * source.shape[1]

    sent, both_z = pl.pallas_call(
        forward_z,
        out_shape=[
            jax.ShapeDtypeStruct((devices, 2, 32, 128), F32),
            jax.ShapeDtypeStruct((2 * n, n), BF16),
        ],
        in_specs=[HBM_SPEC] * 2,
        out_specs=[VMEM_SPEC] * 2,
        scratch_shapes=[
            pltpu.VMEM((lines, n), F32),
            pltpu.VMEM(square, F32),
            pltpu.VMEM((2, lines * 2, 128), F32),
            pltpu.SemaphoreType.DMA((lines // 512 + 1,)),
        ],
        compiler_params=limit(20),
        name="forward_z",
    )(in_hbm(source.reshape(lines, n)), in_hbm(basis_z))
    sent = sent.reshape(devices, 64, 128)
    field = lax.all_to_all(sent, AXES, split_axis=0, concat_axis=0, tiled=True)

    shape = (rows_n, cols_n, 4, 16, 128)
    field = pl.pallas_call(
        planes,
        out_shape=jax.ShapeDtypeStruct(shape, F32),
        in_specs=[VMEM_SPEC] * 5 + [pl.BlockSpec(memory_space=pltpu.SMEM)],
        out_specs=VMEM_SPEC,
        scratch_shapes=[pltpu.VMEM((n // 128, n, 128), F32)]
        + [pltpu.VMEM(square, BF16)] * 8
        + [pltpu.VMEM((n, 128), F32)]
        + [pltpu.VMEM((2,) + square, BF16)] * 2,
        compiler_params=limit(24),
        name="planes",
    )(
        field.reshape(rows_n, cols_n, 2, 4, 8, 128), basis_x, basis_y,
        eigen_x.reshape(1, n), eigen_y.reshape(1, n), eigen_z,
    )

    field = field.reshape(devices, 64, 128)
    field = lax.all_to_all(field, AXES, split_axis=0, concat_axis=0, tiled=True)
    out = pl.pallas_call(
        backward_z,
        out_shape=jax.ShapeDtypeStruct((lines, n), F32),
        in_specs=[VMEM_SPEC] * 2,
        out_specs=HBM_SPEC,
        scratch_shapes=[
            pltpu.VMEM((2, lines * 2, 128), F32),
            pltpu.VMEM((lines, n), F32),
            pltpu.SemaphoreType.DMA((lines // 256,)),
        ],
        compiler_params=limit(20),
        name="backward_z",
    )(field.reshape(devices, 4, 16, 128), both_z)
    return out.reshape(source.shape)


def solution(mesh):
    placed = (P("row", "col", None), P(), P(), P(), P(), P(), P())
    return jax.shard_map(
        local, mesh=mesh, in_specs=placed, out_specs=P("row", "col", None), check_vma=False
    )
```

time: 150 us -> 147 us (0.980)
  blocking collectives: 57.9 us -> 121 us
  waiting for transfers between devices: 47.6 us -> 0 us
  starting transfers between devices: 12 us -> 0 us
  Pallas kernels: 32.1 us -> 25.4 us
    all_to_all x0 -> x1, blocking collectives: none -> 63.3 us  [local(): field = lax.all_to_all(sent, AXES, split_axis=0, concat_axis=0, tiled=True)]
    all_to_all x1 -> x0, waiting for transfers between devices: 47.6 us -> none  [local(): field = lax.all_to_all(sent, AXES, split_axis=0, concat_axis=0, tiled=True)]
    all_to_all x1 -> x0, starting transfers between devices: 12 us -> none  [local(): field = lax.all_to_all(sent, AXES, split_axis=0, concat_axis=0, tiled=True)]
    pallas_call x1 -> x0, Pallas kernels: 3.97 us -> none  [local(): pl.pallas_call(prepare, out_shape=[table] * 8 + [jax.ShapeDtypeStruct((n,...]
    pallas_call x1, Pallas kernels: 16.3 us -> 14.5 us  [local(): pl.pallas_call(planes, out_shape=jax.ShapeDtypeStruct(shape, F32), in_spe...]
  transfers between devices with their start and end apart: 1 -> 0, of which waited for: 1 -> 0; matrix products, arithmetic and copies ran while one was open for 0% -> 0% of each run, Pallas kernels for 3% -> 0%
where the time goes in v4:
time: 147 us
  blocking collectives  121 us (82%)
  Pallas kernels  25.4 us (17%)
    all_to_all x1, blocking collectives, local(): field = lax.all_to_all(sent, AXES, split_axis=0, concat_axis=0, tiled=True)  63.3 us
    all_to_all x1, blocking collectives, local(): field = lax.all_to_all(field, AXES, split_axis=0, concat_axis=0, tiled=True)  57.9 us
    pallas_call x1, Pallas kernels, local(): pl.pallas_call(planes, out_shape=jax.ShapeDtypeStruct(shape, F32), in_spe...  14.5 us
    pallas_call x1, Pallas kernels, local(): pl.pallas_call(forward_z, out_shape=[jax.ShapeDtypeStruct((devices, 2, 32...  6.17 us
    pallas_call x1, Pallas kernels, local(): pl.pallas_call(backward_z, out_shape=jax.ShapeDtypeStruct((lines, n), F32...  4.74 us

profile of v4, /device:TPU:1, one launch (start us, length us, event | category | flops | bytes accessed | tf_op | source)
XLA Modules:
  0.0 146.8 jit_solution(15738083715845931408)
XLA Ops:
  0.0 6.2 %forward_z.1 = (f32[128,2,32,128]{3,2,1,0:T(8,128)S(1)}, bf16[1024,512]{1,0:T(8,128)(2,1)S(1)}) custom-call(f32[2048,512]{1,0:T(8,128)} %bitcast.14, f32[512,512]{1,0:T(8,128)} %basis_hbm.1), custom_call_target="tpu_custom_call" | custom-call | tf_op jit(solution)/shard_map/forward_z/pallas_call | solution.py:201
  6.2 0.0 copy-start
  6.2 0.0 copy-start.1
  6.2 0.0 copy-start.2
  6.2 0.0 copy-start.3
  6.2 0.0 copy-start.4
  6.2 63.3 %all_to_all.10 = f32[128,64,128]{2,1,0:T(8,128)S(1)} all-to-all(f32[128,64,128]{2,1,0:T(8,128)S(1)} %bitcast.11), channel_id=1, replica_groups=mesh['row'=16,'col'=8] {'row','col'}, dimensions={0} | all-to-all | bytes 8388608 | tf_op jit(solution)/shard_map/all_to_all | solution.py:219
  69.5 0.0 copy-done
  69.5 0.0 copy-done.1
  69.5 0.0 copy-done.2
  69.5 0.0 copy-done.3
  69.5 0.0 copy-done.4
  69.5 14.5 %planes.1 = f32[16,8,4,16,128]{4,3,2,1,0:T(8,128)S(1)} custom-call(f32[16,8,2,4,8,128]{5,4,3,2,1,0:T(8,128)S(1)} %bitcast.9, f32[512,512]{1,0:T(8,128)S(1)} %copy-done, f32[512,512]{1,0:T(8,128)S(1)} %copy-done.1, f32[1,512]{1,0:T(1,128)S(1)} %bitcast.12, f32[1,512]{1,0:T(1,128)S(1)} %bitcast.13, f32[512]{0:T(512)S(1)} %copy-done.4), custom_call_target="tpu_custom_call" | custom-call | tf_op jit(solution)/shard_map/planes/pallas_call | solution.py:222
  84.0 57.9 %all_to_all.11 = f32[128,64,128]{2,1,0:T(8,128)S(1)} all-to-all(f32[128,64,128]{2,1,0:T(8,128)S(1)} %bitcast.10), channel_id=1, replica_groups=mesh['row'=16,'col'=8] {'row','col'}, dimensions={0} | all-to-all | bytes 8388608 | tf_op jit(solution)/shard_map/all_to_all | solution.py:239
  141.9 4.7 %backward_z.1 = f32[2048,512]{1,0:T(8,128)} custom-call(f32[128,4,16,128]{3,2,1,0:T(8,128)S(1)} %bitcast.8, bf16[1024,512]{1,0:T(8,128)(2,1)S(1)} %get-tuple-element.8.both_ref), custom_call_target="tpu_custom_call" | custom-call | tf_op jit(solution)/shard_map/backward_z/pallas_call | solution.py:240
Async XLA Ops:
  6.2 63.3 %copy-start = (f32[512,512]{1,0:T(8,128)S(1)}, f32[512,512]{1,0:T(8,128)}, u32[]{:S(2)}) copy-start(f32[512,512]{1,0:T(8,128)} %basis_x.1) | copy-start | bytes 3145732
  6.2 63.3 %copy-start.1 = (f32[512,512]{1,0:T(8,128)S(1)}, f32[512,512]{1,0:T(8,128)}, u32[]{:S(2)}) copy-start(f32[512,512]{1,0:T(8,128)} %basis_y.1) | copy-start | bytes 3145732
  6.2 63.3 %copy-start.2 = (f32[512]{0:T(512)S(1)}, f32[512]{0:T(512)}, u32[]{:S(2)}) copy-start(f32[512]{0:T(512)} %param.11) | copy-start | bytes 6148
  6.2 63.3 %copy-start.3 = (f32[512]{0:T(512)S(1)}, f32[512]{0:T(512)}, u32[]{:S(2)}) copy-start(f32[512]{0:T(512)} %param.12) | copy-start | bytes 6148
  6.2 63.3 %copy-start.4 = (f32[512]{0:T(512)S(1)}, f32[512]{0:T(512)}, u32[]{:S(2)}) copy-start(f32[512]{0:T(512)} %eigen_z.1) | copy-start | bytes 6148

commit v5 on v4

--- a/solution.py
+++ b/solution.py
@@ -94,6 +94,10 @@
     owned = (lax.axis_index("row") * cols_n + lax.axis_index("col")) * count
     lower = lax.broadcasted_iota(jnp.int32, (half, 128), 1) < 64
 
+    def trade(one, other):
+        moved = pltpu.roll(jnp.where(lower, other, one), 64, 1)
+        return jnp.where(lower, one, moved), jnp.where(lower, moved, other)
+
     def ordered(strip):
         return jnp.concatenate(
             [strips[strip, pl.ds(side, n // 2, stride=2), :] for side in range(2)], axis=0
@@ -121,8 +125,7 @@
         for pair in range(cols_n // 2):
             left = field_ref[:, 2 * pair, :, plane].reshape(half, 128)
             right = field_ref[:, 2 * pair + 1, :, plane].reshape(half, 128)
-            even = jnp.where(lower, left, pltpu.roll(right, 64, 1))
-            odd = jnp.where(lower, pltpu.roll(left, 64, 1), right)
+            even, odd = trade(left, right)
             at = pl.ds(pair * 128, 128)
             for rows, value in ((pl.ds(0, half), even), (pl.ds(half, half), odd)):
                 plane_high[side, rows, at], plane_low[side, rows, at] = halves(value)
@@ -131,8 +134,7 @@
         for pair in range(cols_n // 2):
             even = field[:half, pair * 128 : pair * 128 + 128]
             odd = field[half:, pair * 128 : pair * 128 + 128]
-            left = jnp.where(lower, even, pltpu.roll(odd, 64, 1))
-            right = jnp.where(lower, pltpu.roll(even, 64, 1), odd)
+            left, right = trade(even, odd)
             out_ref[:, 2 * pair, plane] = left.reshape(rows_n, 16, 128)
             out_ref[:, 2 * pair + 1, plane] = right.reshape(rows_n, 16, 128)
 

time: 147 us -> 147 us (level)
  no operation moved by 1% of the time
where the time goes in v5:
time: 147 us
  blocking collectives  121 us (82%)
  Pallas kernels  25.4 us (17%)
    all_to_all x1, blocking collectives, local(): field = lax.all_to_all(sent, AXES, split_axis=0, concat_axis=0, tiled=True)  63.3 us
    all_to_all x1, blocking collectives, local(): field = lax.all_to_all(field, AXES, split_axis=0, concat_axis=0, tiled=True)  57.9 us
    pallas_call x1, Pallas kernels, local(): pl.pallas_call(planes, out_shape=jax.ShapeDtypeStruct(shape, F32), in_spe...  14.5 us
    pallas_call x1, Pallas kernels, local(): pl.pallas_call(forward_z, out_shape=[jax.ShapeDtypeStruct((devices, 2, 32...  6.17 us
    pallas_call x1, Pallas kernels, local(): pl.pallas_call(backward_z, out_shape=jax.ShapeDtypeStruct((lines, n), F32...  4.74 us

profile of v5, /device:TPU:1, one launch (start us, length us, event | category | flops | bytes accessed | tf_op | source)
XLA Modules:
  0.0 146.9 jit_solution(5607266684057736596)
XLA Ops:
  0.0 6.2 %forward_z.1 = (f32[128,2,32,128]{3,2,1,0:T(8,128)S(1)}, bf16[1024,512]{1,0:T(8,128)(2,1)S(1)}) custom-call(f32[2048,512]{1,0:T(8,128)} %bitcast.14, f32[512,512]{1,0:T(8,128)} %basis_hbm.1), custom_call_target="tpu_custom_call" | custom-call | tf_op jit(solution)/shard_map/forward_z/pallas_call | solution.py:203
  6.2 0.0 copy-start
  6.2 0.0 copy-start.1
  6.2 0.0 copy-start.2
  6.2 0.0 copy-start.3
  6.2 0.0 copy-start.4
  6.2 63.3 %all_to_all.10 = f32[128,64,128]{2,1,0:T(8,128)S(1)} all-to-all(f32[128,64,128]{2,1,0:T(8,128)S(1)} %bitcast.11), channel_id=1, replica_groups=mesh['row'=16,'col'=8] {'row','col'}, dimensions={0} | all-to-all | bytes 8388608 | tf_op jit(solution)/shard_map/all_to_all | solution.py:221
  69.5 0.0 copy-done
  69.5 0.0 copy-done.1
  69.5 0.0 copy-done.2
  69.5 0.0 copy-done.3
  69.5 0.0 copy-done.4
  69.5 14.5 %planes.1 = f32[16,8,4,16,128]{4,3,2,1,0:T(8,128)S(1)} custom-call(f32[16,8,2,4,8,128]{5,4,3,2,1,0:T(8,128)S(1)} %bitcast.9, f32[512,512]{1,0:T(8,128)S(1)} %copy-done, f32[512,512]{1,0:T(8,128)S(1)} %copy-done.1, f32[1,512]{1,0:T(1,128)S(1)} %bitcast.12, f32[1,512]{1,0:T(1,128)S(1)} %bitcast.13, f32[512]{0:T(512)S(1)} %copy-done.4), custom_call_target="tpu_custom_call" | custom-call | tf_op jit(solution)/shard_map/planes/pallas_call | solution.py:224
  84.1 57.9 %all_to_all.11 = f32[128,64,128]{2,1,0:T(8,128)S(1)} all-to-all(f32[128,64,128]{2,1,0:T(8,128)S(1)} %bitcast.10), channel_id=1, replica_groups=mesh['row'=16,'col'=8] {'row','col'}, dimensions={0} | all-to-all | bytes 8388608 | tf_op jit(solution)/shard_map/all_to_all | solution.py:241
  141.9 4.7 %backward_z.1 = f32[2048,512]{1,0:T(8,128)} custom-call(f32[128,4,16,128]{3,2,1,0:T(8,128)S(1)} %bitcast.8, bf16[1024,512]{1,0:T(8,128)(2,1)S(1)} %get-tuple-element.8.both_ref), custom_call_target="tpu_custom_call" | custom-call | tf_op jit(solution)/shard_map/backward_z/pallas_call | solution.py:242
Async XLA Ops:
  6.2 63.3 %copy-start = (f32[512,512]{1,0:T(8,128)S(1)}, f32[512,512]{1,0:T(8,128)}, u32[]{:S(2)}) copy-start(f32[512,512]{1,0:T(8,128)} %basis_x.1) | copy-start | bytes 3145732
  6.2 63.3 %copy-start.1 = (f32[512,512]{1,0:T(8,128)S(1)}, f32[512,512]{1,0:T(8,128)}, u32[]{:S(2)}) copy-start(f32[512,512]{1,0:T(8,128)} %basis_y.1) | copy-start | bytes 3145732
  6.2 63.3 %copy-start.2 = (f32[512]{0:T(512)S(1)}, f32[512]{0:T(512)}, u32[]{:S(2)}) copy-start(f32[512]{0:T(512)} %param.11) | copy-start | bytes 6148
  6.2 63.3 %copy-start.3 = (f32[512]{0:T(512)S(1)}, f32[512]{0:T(512)}, u32[]{:S(2)}) copy-start(f32[512]{0:T(512)} %param.12) | copy-start | bytes 6148
  6.2 63.3 %copy-start.4 = (f32[512]{0:T(512)S(1)}, f32[512]{0:T(512)}, u32[]{:S(2)}) copy-start(f32[512]{0:T(512)} %eigen_z.1) | copy-start | bytes 6148
